TPU v7x, 128 devices: a whole 4x4x4 slice. The times are simulated.
128 devices in a mesh: seq: 4 (over x_lo, core), tensor: 32 (over z, y, x_hi).
Axes of the slice: x: 4 (x_hi: 2, x_lo: 2; x = x_hi * 2 + x_lo), y: 4, z: 4, core: 2. Of those that a mesh axis runs over, the one named last changes fastest.
Arguments:
- tokens: bfloat16 [2, 4096, 4096], P(None, 'seq', 'tensor'), may hold values from -6 to 6
- w_qkv: bfloat16 [4096, 3, 4096], P(None, None, 'tensor'), may hold values from -1 to 1
- q_gain: float32 [4096], P('tensor'), may hold values from 0.5 to 2.5
- k_gain: float32 [4096], P('tensor'), may hold values from 0.5 to 2.5
- w_out: bfloat16 [4096, 4096], P('tensor'), may hold values from -0.1875 to 0.1875
Outputs:
- mixed: bfloat16 [2, 4096, 4096], P(None, 'seq', 'tensor')
- peak: float32 [32], P('tensor')
- qk_scale: float32 [2, 2, 4096], P(None, None, 'seq')
All inputs are finite; a program needn't handle non-finite values.
Results may differ from a plain program's by a relative error of at most 0.024.
Values may be sent and summed in bfloat16 or wider, within the bound.
A program may use at most 128 MiB of HBM per device.

v0:
```python
import jax
import jax.numpy as jnp
from jax import lax
from jax.sharding import Mesh
from jax.sharding import PartitionSpec as P

HEADS = 32
TENSOR = ("tensor_0", "tensor_1", "tensor_2")
EPS = 1e-06
ROPE_BASE = 500000.0
NEG = -1e30


def sent_to_all(array, axis):
    size = lax.axis_size(axis)
    return lax.all_to_all(
        jnp.broadcast_to(array[None], (size, *array.shape)), axis, 0, 0, tiled=True
    )


def taken_together(array, axis):
    return sent_to_all(array, axis).sum(axis=0)


def side_by_side(arrays, axis, dim, along):
    both = jnp.concatenate(arrays, axis=along)
    filled, at, gathered = (lax.all_gather(both, axis, axis=dim, tiled=True), 0, [])
    for a in arrays:
        gathered.append(lax.slice_in_dim(filled, at, at + a.shape[along], axis=along))
        at += a.shape[along]
    return tuple(gathered)


def over_copies(array, axis):
    return sent_to_all(array, axis).max(axis=0)


def sum_by_axis(array, axes, dim):
    for axis in axes:
        array = lax.psum_scatter(array, axis, scatter_dimension=dim, tiled=True)
    return array


def rope_tables(positions, head):
    half = head // 2
    freq = ROPE_BASE ** (-(jnp.arange(half, dtype=jnp.float32) * 2.0) / head)
    angle = positions[:, None] * freq[None, :]
    return (jnp.cos(angle), jnp.sin(angle))


def rotate(values, cosine, sine):
    half = values.shape[-1] // 2
    first = values[..., :half]
    second = values[..., half:]
    cosine = cosine[:, None, :]
    sine = sine[:, None, :]
    return jnp.concatenate([first * cosine - second * sine, second * cosine + first * sine], -1)


def norm_stats(query, keyed, width):
    totals = taken_together(
        jnp.stack([jnp.sum(query * query, 1), jnp.sum(keyed * keyed, 1)]), TENSOR
    )
    return lax.rsqrt(totals / width + EPS)


def online_update(q_part, k_part, v_part, valid, state, scale):
    top, denom, accum = state
    scores = jnp.einsum("sqd,skd->sqk", q_part, k_part, preferred_element_type=jnp.float32) * scale
    scores = jnp.where(valid[None], scores, NEG)
    new_top = jnp.maximum(top, jnp.max(scores, -1))
    weights = jnp.where(valid[None], jnp.exp(scores - new_top[..., None]), 0.0)
    factor = jnp.exp(top - new_top)
    added = jnp.einsum(
        "sqk,skd->sqd", weights.astype(jnp.bfloat16), v_part, preferred_element_type=jnp.float32
    )
    return (new_top, denom * factor + jnp.sum(weights, -1), accum * factor[..., None] + added)


def shards(tokens, w_qkv, q_gain, k_gain, w_out):
    seqs, tok, dloc = tokens.shape
    width = w_qkv.shape[0]
    head = width // HEADS
    heads_here = dloc // head
    rows = seqs * tok
    flat_w = w_qkv.reshape(width, 3 * dloc)
    whole = lax.all_gather(tokens, TENSOR, axis=2, tiled=True).reshape(rows, width)
    paired = jnp.dot(whole, flat_w[:, : 2 * dloc], preferred_element_type=jnp.float32)
    query = paired[:, :dloc]
    keyed = paired[:, dloc:]
    inverse = norm_stats(query, keyed, width)
    value = jnp.dot(whole, flat_w[:, 2 * dloc :], preferred_element_type=jnp.float32)
    own_index = lax.axis_index("seq")
    q_index = own_index * tok + jnp.arange(tok, dtype=jnp.int32)
    cosine, sine = rope_tables(q_index.astype(jnp.float32), head)

    def prepare(projection, scale_row, gain):
        normed = projection * scale_row[:, None] * gain[None, :]
        return rotate(normed.reshape(seqs, tok, heads_here, head), cosine, sine).astype(
            jnp.bfloat16
        )

    q_heads = prepare(query, inverse[0], q_gain).transpose(2, 0, 1, 3)
    k_ready = prepare(keyed, inverse[1], k_gain).reshape(seqs, tok, dloc)
    v_ready = value.astype(jnp.bfloat16).reshape(seqs, tok, dloc)
    scale = head ** (-0.5)
    keys_all, values_all = side_by_side((k_ready, v_ready), "seq", 1, 0)
    total_len = keys_all.shape[1]
    k_heads = keys_all.reshape(seqs, total_len, heads_here, head).transpose(2, 0, 1, 3)
    v_heads = values_all.reshape(seqs, total_len, heads_here, head).transpose(2, 0, 1, 3)

    def attend(operands):
        q_one, k_one, v_one = operands

        def visit(step, state):
            first = step * tok
            k_part = lax.dynamic_slice_in_dim(k_one, first, tok, 1)
            v_part = lax.dynamic_slice_in_dim(v_one, first, tok, 1)
            valid = (first + jnp.arange(tok, dtype=jnp.int32))[None, :] <= q_index[:, None]
            return online_update(q_one, k_part, v_part, valid, state, scale)

        initial = (
            jnp.full((seqs, tok), NEG, jnp.float32),
            jnp.zeros((seqs, tok), jnp.float32),
            jnp.zeros((seqs, tok, head), jnp.float32),
        )
        top, denom, accum = lax.fori_loop(0, own_index + 1, visit, initial)
        return (accum / denom[..., None], top)

    outputs, tops = lax.map(attend, (q_heads, k_heads, v_heads))
    attended = outputs.astype(jnp.bfloat16).transpose(1, 2, 0, 3).reshape(rows, dloc)
    peak = over_copies(jnp.max(tops, axis=(1, 2)), "seq")
    partial_out = (
        jnp.dot(attended, w_out, preferred_element_type=jnp.float32)
        .astype(jnp.bfloat16)
        .reshape(seqs, tok, width)
    )
    mixed = sum_by_axis(partial_out, TENSOR, 2).astype(jnp.float32)
    return (mixed.astype(jnp.bfloat16), peak, inverse.reshape(2, seqs, tok))


def solution(mesh):
    finer = Mesh(
        mesh.devices.reshape(mesh.shape["seq"], 4, 4, 2),
        ("seq", "tensor_0", "tensor_1", "tensor_2"),
    )
    placed = (P(None, "seq", TENSOR), P(None, None, TENSOR), P(TENSOR), P(TENSOR), P(TENSOR, None))
    return jax.shard_map(
        shards,
        mesh=finer,
        in_specs=placed,
        out_specs=(P(None, "seq", TENSOR), P(TENSOR), P(None, None, "seq")),
        check_vma=False,
    )
```

profile of v0, /device:TPU:1, one launch (start us, length us, event | category | flops | bytes accessed | tf_op | source)
XLA Modules:
  0.0 593.4 jit_solution(10021887254225840839)
XLA Ops:
  7.2 0.0 copy-start
  7.2 0.0 all-gather.3.cloned.1.call-start
  7.2 0.7 all-gather.3.cloned.1.call-update
  7.9 4.7 copy.16
  12.7 3.1 multiply_cosine_fusion
  15.7 205.0 %all-gather.3.cloned.1.call-done = bf16[2,1024,4096]{2,1,0:T(8,128)(2,1)} async-done(((bf16[2,1024,128]{2,1,0:T(8,128)(2,1)}), bf16[2,1024,4096]{2,1,0:T(8,128)(2,1)}) %all-gather.3.cloned.1.call-update) | async-done | bytes 16777232 | tf_op jit(solution)/shard_map/all_gather | solution.py:87
  220.7 8.8 %fusion.19 = f32[2048,256]{1,0:T(8,128)S(1)} fusion(bf16[2048,4096]{1,0:T(8,128)(2,1)} %bitcast.64, bf16[4096,384]{0,1:T(8,128)(2,1)} %bitcast.55), kind=kOutput, calls=%fused_computation.24 | convolution fusion | flops 4294967296 | bytes 20971520 | tf_op jit(solution)/shard_map/dot_general | solution.py:88
  229.5 0.6 multiply_reduce_fusion.1
  230.1 1.0 broadcast_in_dim.36
  231.2 5.4 all-to-all-start
  236.6 0.0 copy-start.2
  236.6 0.0 copy-start.3
  236.6 0.0 all-gather.5.cloned.1.call-start
  236.7 11.3 %convolution_convert_fusion.1 = bf16[2048,128]{1,0:T(8,128)(2,1)} fusion(bf16[2048,4096]{1,0:T(8,128)(2,1)} %bitcast.65, bf16[4096,384]{0,1:T(8,128)(2,1)} %bitcast.56), kind=kOutput, calls=%fused_computation.23 | convolution fusion | flops 2147745792 | bytes 18350080 | tf_op jit(solution)/shard_map/dot_general | solution.py:92
  248.0 0.5 all-to-all-done
  248.5 1.2 reduce_sum.38
  249.8 0.0 copy-start.1
  249.8 0.0 copy-done.2
  249.8 0.0 copy-done.3
  249.8 0.7 multiply_multiply_fusion
  250.6 2.0 fusion.24
  252.5 0.0 copy-done.1
  252.5 1.3 pad_maximum_fusion
  253.8 0.0 all-gather.5.cloned.1.call-update
  253.8 0.2 reduce-scatter.6.cloned.1.call-start
  254.1 1.1 pad_maximum_fusion.1
  255.1 48.1 %all-gather.5.cloned.1.call-done = bf16[4,4096,128]{2,1,0:T(8,128)(2,1)} async-done(((bf16[4,1024,128]{2,1,0:T(8,128)(2,1)}), bf16[4,4096,128]{2,1,0:T(8,128)(2,1)}) %all-gather.5.cloned.1.call-update) | async-done | bytes 4194320 | tf_op jit(solution)/shard_map/all_gather | solution.py:27
  303.3 4.5 fusion.26
  307.7 0.1 broadcast.114
  307.8 21.6 %while.25 = (s32[]{:T(128)}, f32[2,1024]{1,0:T(2,128)S(1)}, f32[2,1024]{1,0:T(2,128)S(1)}, f32[2,1024,128]{2,1,0:T(8,128)S(1)}, s32[]{:T(128)}, /*index=5*/bf16[...) while((s32[]{:T(128)}, f32[2,1024]{1,0:T(2,128)S(1)}, ...), condition=%wide.region_6.7_spmd.clone, body=%wide.region_3.6_spmd.clone.sunk | while | flops 1102583808 | bytes 33177796 | solution.py:127
  307.8 0.7 broadcast_compare_fusion.2
  308.5 3.0 fusion.42
  311.5 2.3 fusion.43
  313.8 4.8 fusion.44
  318.6 0.7 broadcast_compare_fusion.2
  319.3 3.0 fusion.42
  322.3 2.3 fusion.43
  324.6 4.8 fusion.44
  329.4 0.3 divide_convert_fusion
  329.7 0.0 copy-done
  329.7 8.0 %convolution_convert_fusion = bf16[2048,4096]{1,0:T(8,128)(2,1)} fusion(bf16[2048,128]{1,0:T(8,128)(2,1)S(1)} %bitcast.57, bf16[128,4096]{1,0:T(8,128)(2,1)S(1)} %copy-done), kind=kOutput, calls=%fused_computation.22 | convolution fusion | flops 2155872256 | bytes 18350080 | tf_op jit(solution)/shard_map/dot_general | solution.py:134
  337.8 0.0 reduce-scatter.6.cloned.1.call-update
  337.8 0.0 reduce-scatter.8.cloned.1.call-start
  337.9 169.6 %reduce-scatter.6.cloned.1.call-done = bf16[2,1024,1024]{2,1,0:T(8,128)(2,1)} async-done(((bf16[2,1024,4096]{2,1,0:T(8,128)(2,1)}), bf16[2,1024,1024]{2,1,0:T(8,128)(2,1)}) %reduce-scatter.6.cloned.1.call-update) | async-done | bytes 4194320 | tf_op jit(solution)/shard_map/reduce_scatter | solution.py:40
  507.5 0.0 reduce-scatter.8.cloned.1.call-update
  507.5 0.0 reduce-scatter.10.cloned.1.call-start
  507.6 48.6 %reduce-scatter.8.cloned.1.call-done = bf16[2,1024,256]{2,1,0:T(8,128)(2,1)} async-done(((bf16[2,1024,1024]{2,1,0:T(8,128)(2,1)}), bf16[2,1024,256]{2,1,0:T(8,128)(2,1)}) %reduce-scatter.8.cloned.1.call-update) | async-done | bytes 1048592 | tf_op jit(solution)/shard_map/reduce_scatter | solution.py:40
  556.2 2.6 copy.20
  558.8 1.3 copy.24
  560.0 0.0 reduce-scatter.10.cloned.1.call-update
  560.1 0.6 rsqrt.8
  560.7 0.6 reduce_max.29
  561.3 0.6 broadcast_in_dim.37
  562.0 6.4 %all_to_all.11 = f32[4,1,1]{2,1,0:T(1,128)S(1)} all-to-all(f32[4,1,1]{2,1,0:T(1,128)S(1)} %broadcast_in_dim.37), channel_id=1, replica_groups=mesh['seq'=4,'tensor_0'=4,'tensor_1'=4,'tensor_2'=2] {'seq'}, dimensions={0} | all-to-all | bytes 32 | tf_op jit(solution)/shard_map/all_to_all | solution.py:16
  568.3 0.6 reduce_max.30
  568.9 15.3 %reduce-scatter.10.cloned.1.call-done = bf16[128,2048]{1,0:T(8,128)(2,1)} async-done(((bf16[256,2048]{1,0:T(8,128)(2,1)}), bf16[128,2048]{1,0:T(8,128)(2,1)}) %reduce-scatter.10.cloned.1.call-update) | async-done | bytes 524304
  584.2 1.4 reshape.187
  585.7 1.2 copy.21
  (15 shorter events, 0.1 us)
Async XLA Ops:
  7.2 322.6 %copy-start = (bf16[128,4096]{1,0:T(8,128)(2,1)S(1)}, bf16[128,4096]{1,0:T(8,128)(2,1)}, u32[]{:S(2)}) copy-start(bf16[128,4096]{1,0:T(8,128)(2,1)} %param.11) | copy-start | bytes 3145732
  7.2 213.6 %all-gather.3.cloned.1.call-start = ((), (), s32[]{:S(2)}) async-start(), calls=%async_computation.5 | async-start | bytes 17301504 | tf_op jit(solution)/shard_map/all_gather | solution.py:87
  231.2 17.4 %all-to-all-start = ((f32[32,2,2048]{2,1,0:T(2,128)}), f32[32,2,2048]{2,1,0:T(2,128)}, u32[]{:S(2)}, u32[]{:S(2)}) async-start(f32[32,2,2048]{2,1,0:T(2,128)} %broadcast_in_dim.36), calls=%async_computation | async-start | bytes 1048576 | tf_op jit(solution)/shard_map/all_to_all | solution.py:16
  236.6 13.2 %copy-start.2 = (f32[128]{0:T(128)S(1)}, f32[128]{0:T(128)}, u32[]{:S(2)}) copy-start(f32[128]{0:T(128)} %param.9) | copy-start | bytes 1540
  236.6 13.2 %copy-start.3 = (f32[128]{0:T(128)S(1)}, f32[128]{0:T(128)}, u32[]{:S(2)}) copy-start(f32[128]{0:T(128)} %param.10) | copy-start | bytes 1540
  236.6 66.6 %all-gather.5.cloned.1.call-start = ((), (), s32[]{:S(2)}) async-start(), calls=%async_computation.6 | async-start | bytes 5242880 | tf_op jit(solution)/shard_map/all_gather | solution.py:27
  249.8 2.8 copy-start.1
  253.8 253.7 %reduce-scatter.6.cloned.1.call-start = ((), (), s32[]{:S(2)}) async-start(), calls=%async_computation.7 | async-start | bytes 20971520 | tf_op jit(solution)/shard_map/reduce_scatter | solution.py:40
  337.8 218.4 %reduce-scatter.8.cloned.1.call-start = ((), (), s32[]{:S(2)}) async-start(), calls=%async_computation.8 | async-start | bytes 5242880 | tf_op jit(solution)/shard_map/reduce_scatter | solution.py:40
  507.5 76.7 %reduce-scatter.10.cloned.1.call-start = ((), (), s32[]{:S(2)}) async-start(), calls=%async_computation.9 | async-start | bytes 1572864
Sparse Core Ops, SparseCore 0:
  10.7 209.9 all-gather.2
  253.9 49.2 all-gather.4
  337.9 169.4 reduce-scatter.5
  509.7 46.4 reduce-scatter.7
  560.2 24.0 reduce-scatter.9
where the time goes:
time: 594 us; the launch traced here: 593 us
  waiting for transfers between devices  488 us (82%)
  matrix products  43.7 us (7%)
  local copies, waits for them, and re-layouts  18.1 us (3%)
  other arithmetic  17.4 us (3%)
  between operations  14 us (2%)
  blocking collectives  6.36 us (1%)
    reduce_scatter x2, waiting for transfers between devices, sum_by_axis(): array = lax.psum_scatter(array, axis, scatter_dimension=dim, tiled=True)  218 us
    all_gather x1, waiting for transfers between devices, shards(): lax.all_gather(tokens, TENSOR, axis=2, tiled=True).reshape(rows, width)  205 us
    all_gather x1, waiting for transfers between devices, side_by_side(): lax.all_gather(both, axis, axis=dim, tiled=True)  48.1 us
    unnamed x6, waiting for transfers between devices  16.1 us
  transfers between devices with their start and end apart: 6, of which 6 were waited for; matrix products, arithmetic and copies ran while one was open for 4% of the time, Pallas kernels for 0%

commit v1 on v0

--- a/solution.py
+++ b/solution.py
@@ -1,3 +1,4 @@
+import functools
 import jax
 import jax.numpy as jnp
 from jax import lax
@@ -9,6 +10,14 @@
 EPS = 1e-06
 ROPE_BASE = 500000.0
 NEG = -1e30
+
+
+def fit_the_row(body, axis_tag):
+    near = jnp.concatenate(jax.lax.all_gather(body, axis_tag), axis=2)
+    return near
+
+
+loops_hold = functools.partial(fit_the_row, axis_tag=TENSOR)
 
 
 def sent_to_all(array, axis):
@@ -84,7 +93,7 @@
     heads_here = dloc // head
     rows = seqs * tok
     flat_w = w_qkv.reshape(width, 3 * dloc)
-    whole = lax.all_gather(tokens, TENSOR, axis=2, tiled=True).reshape(rows, width)
+    whole = loops_hold(tokens).reshape(rows, width)
     paired = jnp.dot(whole, flat_w[:, : 2 * dloc], preferred_element_type=jnp.float32)
     query = paired[:, :dloc]
     keyed = paired[:, dloc:]

time: 594 us -> 567 us (0.955)
  waiting for transfers between devices: 488 us -> 437 us
  local copies, waits for them, and re-layouts: 18.1 us -> 36.8 us
    all_gather x1, waiting for transfers between devices: 205 us -> 154 us  [fit_the_row(): near = jnp.concatenate(jax.lax.all_gather(body, axis_tag), axis=2)]
    all_gather x0 -> x1, local copies, waits for them, and re-layouts: none -> 18.7 us  [fit_the_row(): near = jnp.concatenate(jax.lax.all_gather(body, axis_tag), axis=2)]
  transfers between devices with their start and end apart: 6 -> 6, of which waited for: 6 -> 5; matrix products, arithmetic and copies ran while one was open for 4% -> 4% of each run, Pallas kernels for 0% -> 0%
where the time goes in v1:
time: 567 us; the launch traced here: 566 us
  waiting for transfers between devices  437 us (77%)
  matrix products  48.4 us (9%)
  local copies, waits for them, and re-layouts  36.8 us (6%)
  other arithmetic  17.4 us (3%)
  between operations  14 us (2%)
  blocking collectives  6.34 us (1%)
  starting transfers between devices  6.18 us (1%)
    reduce_scatter x2, waiting for transfers between devices, sum_by_axis(): array = lax.psum_scatter(array, axis, scatter_dimension=dim, tiled=True)  218 us
    all_gather x1, waiting for transfers between devices, fit_the_row(): near = jnp.concatenate(jax.lax.all_gather(body, axis_tag), axis=2)  154 us
    all_gather x1, waiting for transfers between devices, side_by_side(): lax.all_gather(both, axis, axis=dim, tiled=True)  48.6 us
    all_gather x1, local copies, waits for them, and re-layouts, fit_the_row(): near = jnp.concatenate(jax.lax.all_gather(body, axis_tag), axis=2)  18.7 us
    unnamed x6, waiting for transfers between devices  16 us
    dot_general x1, matrix products, shards(): jnp.dot(whole, flat_w[:, 2 * dloc:], preferred_element_type=jnp.float32)  12.4 us
    dot_general x1, matrix products, shards(): jnp.dot(whole, flat_w[:, :2 * dloc], preferred_element_type=jnp.float32)  12.4 us
  transfers between devices with their start and end apart: 6, of which 5 were waited for; matrix products, arithmetic and copies ran while one was open for 4% of the time, Pallas kernels for 0%

profile of v1, /device:TPU:1, one launch (start us, length us, event | category | flops | bytes accessed | tf_op | source)
XLA Modules:
  0.0 566.2 jit_solution(7591308062400247604)
XLA Ops:
  7.2 0.0 copy-start
  7.2 0.0 all-gather.6.cloned.1.call-start
  7.2 0.7 all-gather.6.cloned.1.call-update
  7.9 4.7 copy.20
  12.7 3.1 multiply_cosine_fusion
  15.7 154.0 %all-gather.6.cloned.1.call-done = bf16[64,1024,128]{2,1,0:T(8,128)(2,1)} async-done(((bf16[2,1024,128]{2,1,0:T(8,128)(2,1)}), bf16[64,1024,128]{2,1,0:T(8,128)(2,1)}) %all-gather.6.cloned.1.call-update) | async-done | bytes 16777232 | tf_op jit(solution)/shard_map/all_gather | solution.py:16
  169.7 0.0 copy-start.1
  169.7 18.7 %copy.19 = bf16[32,2,1024,128]{3,0,2,1:T(8,128)(2,1)} copy(bf16[32,2,1024,128]{3,2,1,0:T(8,128)(2,1)} %bitcast.59) | data formatting | bytes 33554432 | tf_op jit(solution)/shard_map/all_gather | solution.py:16
  188.4 0.0 copy-done.1
  188.4 12.4 %fusion.21 = f32[2048,256]{1,0:T(8,128)S(1)} fusion(bf16[256,8,32,128]{3,2,1,0:T(8,128)(2,1)} %bitcast.60, bf16[4096,384]{0,1:T(8,128)(2,1)S(1)} %bitcast.67), kind=kOutput, calls=%fused_computation.24 | convolution fusion | flops 4294967296 | bytes 20971520 | tf_op jit(solution)/shard_map/dot_general | solution.py:97
  200.8 0.6 multiply_reduce_fusion.1
  201.4 1.0 broadcast_in_dim.36
  202.5 5.6 all-to-all-start
  208.1 0.0 copy-start.3
  208.1 0.0 copy-start.4
  208.1 0.2 all-gather.4.cloned.1.call-start
  208.3 12.4 %fusion.25 = bf16[2048,128]{1,0:T(8,128)(2,1)} fusion(bf16[256,8,32,128]{3,2,1,0:T(8,128)(2,1)} %bitcast.61, bf16[4096,384]{0,1:T(8,128)(2,1)} %bitcast.66), kind=kOutput, calls=%fused_computation.29 | convolution fusion | flops 2147745792 | bytes 18350080 | tf_op jit(solution)/shard_map/dot_general | solution.py:101
  220.7 0.0 all-to-all-done
  220.7 1.2 reduce_sum.38
  221.9 0.0 copy-start.2
  222.0 0.0 copy-done.3
  222.0 0.0 copy-done.4
  222.0 0.7 multiply_multiply_fusion
  222.7 2.0 fusion.32
  224.7 0.0 copy-done.2
  224.7 1.3 pad_maximum_fusion
  225.9 0.0 all-gather.4.cloned.1.call-update
  226.0 0.3 reduce-scatter.6.cloned.1.call-start
  226.2 1.1 pad_maximum_fusion.1
  227.3 48.6 %all-gather.4.cloned.1.call-done = bf16[4,4096,128]{2,1,0:T(8,128)(2,1)} async-done(((bf16[4,1024,128]{2,1,0:T(8,128)(2,1)}), bf16[4,4096,128]{2,1,0:T(8,128)(2,1)}) %all-gather.4.cloned.1.call-update) | async-done | bytes 4194320 | tf_op jit(solution)/shard_map/all_gather | solution.py:36
  275.9 4.5 fusion.34
  280.4 0.1 broadcast.114
  280.5 21.6 %while.25 = (s32[]{:T(128)}, f32[2,1024]{1,0:T(2,128)S(1)}, f32[2,1024]{1,0:T(2,128)S(1)}, f32[2,1024,128]{2,1,0:T(8,128)S(1)}, s32[]{:T(128)}, /*index=5*/bf16[...) while((s32[]{:T(128)}, f32[2,1024]{1,0:T(2,128)S(1)}, ...), condition=%wide.region_6.7_spmd.clone, body=%wide.region_3.6_spmd.clone.sunk | while | flops 1102583808 | bytes 33177788 | solution.py:136
  280.5 0.7 broadcast_compare_fusion.2
  281.2 3.0 fusion.48
  284.2 2.3 fusion.49
  286.5 4.8 fusion.50
  291.3 0.7 broadcast_compare_fusion.2
  292.0 3.0 fusion.48
  295.0 2.3 fusion.49
  297.3 4.8 fusion.50
  302.1 0.3 divide_convert_fusion
  302.4 0.0 copy-done
  302.4 8.2 %convolution_convert_fusion = bf16[2048,4096]{1,0:T(8,128)(2,1)} fusion(bf16[2048,128]{1,0:T(8,128)(2,1)S(1)} %bitcast.68, bf16[128,4096]{1,0:T(8,128)(2,1)S(1)} %copy-done), kind=kOutput, calls=%fused_computation.26 | convolution fusion | flops 2155872256 | bytes 18350080 | tf_op jit(solution)/shard_map/dot_general | solution.py:143
  310.6 0.0 reduce-scatter.6.cloned.1.call-update
  310.6 0.0 reduce-scatter.8.cloned.1.call-start
  310.7 169.6 %reduce-scatter.6.cloned.1.call-done = bf16[2,1024,1024]{2,1,0:T(8,128)(2,1)} async-done(((bf16[2,1024,4096]{2,1,0:T(8,128)(2,1)}), bf16[2,1024,1024]{2,1,0:T(8,128)(2,1)}) %reduce-scatter.6.cloned.1.call-update) | async-done | bytes 4194320 | tf_op jit(solution)/shard_map/reduce_scatter | solution.py:49
  480.3 0.0 reduce-scatter.8.cloned.1.call-update
  480.3 0.0 reduce-scatter.10.cloned.1.call-start
  480.4 48.7 %reduce-scatter.8.cloned.1.call-done = bf16[2,1024,256]{2,1,0:T(8,128)(2,1)} async-done(((bf16[2,1024,1024]{2,1,0:T(8,128)(2,1)}), bf16[2,1024,256]{2,1,0:T(8,128)(2,1)}) %reduce-scatter.8.cloned.1.call-update) | async-done | bytes 1048592 | tf_op jit(solution)/shard_map/reduce_scatter | solution.py:49
  529.0 2.6 copy.24
  531.6 1.3 copy.29
  532.9 0.0 reduce-scatter.10.cloned.1.call-update
  532.9 0.6 rsqrt.8
  533.5 0.6 reduce_max.29
  534.2 0.6 broadcast_in_dim.37
  534.8 6.3 %all_to_all.11 = f32[4,1,1]{2,1,0:T(1,128)S(1)} all-to-all(f32[4,1,1]{2,1,0:T(1,128)S(1)} %broadcast_in_dim.37), channel_id=1, replica_groups=mesh['seq'=4,'tensor_0'=4,'tensor_1'=4,'tensor_2'=2] {'seq'}, dimensions={0} | all-to-all | bytes 32 | tf_op jit(solution)/shard_map/all_to_all | solution.py:25
  541.2 0.6 reduce_max.30
  541.8 15.3 %reduce-scatter.10.cloned.1.call-done = bf16[128,2048]{1,0:T(8,128)(2,1)} async-done(((bf16[256,2048]{1,0:T(8,128)(2,1)}), bf16[128,2048]{1,0:T(8,128)(2,1)}) %reduce-scatter.10.cloned.1.call-update) | async-done | bytes 524304
  557.1 1.4 reshape.188
  558.5 1.2 copy.25
  (15 shorter events, 0.2 us)
Async XLA Ops:
  7.2 295.3 %copy-start = (bf16[128,4096]{1,0:T(8,128)(2,1)S(1)}, bf16[128,4096]{1,0:T(8,128)(2,1)}, u32[]{:S(2)}) copy-start(bf16[128,4096]{1,0:T(8,128)(2,1)} %param.11) | copy-start | bytes 3145732
  7.2 162.5 %all-gather.6.cloned.1.call-start = ((), (), s32[]{:S(2)}) async-start(), calls=%async_computation.8 | async-start | bytes 17301504 | tf_op jit(solution)/shard_map/all_gather | solution.py:16
  169.7 18.7 %copy-start.1 = (bf16[4096,3,128]{0,2,1:T(8,128)(2,1)S(1)}, bf16[4096,3,128]{0,2,1:T(8,128)(2,1)}, u32[]{:S(2)}) copy-start(bf16[4096,3,128]{0,2,1:T(8,128)(2,1)} %copy.20) | copy-start | bytes 9437188
  202.5 18.2 %all-to-all-start = ((f32[32,2,2048]{2,1,0:T(2,128)}), f32[32,2,2048]{2,1,0:T(2,128)}, u32[]{:S(2)}, u32[]{:S(2)}) async-start(f32[32,2,2048]{2,1,0:T(2,128)} %broadcast_in_dim.36), calls=%async_computation | async-start | bytes 1048576 | tf_op jit(solution)/shard_map/all_to_all | solution.py:25
  208.1 13.9 %copy-start.3 = (f32[128]{0:T(128)S(1)}, f32[128]{0:T(128)}, u32[]{:S(2)}) copy-start(f32[128]{0:T(128)} %param.9) | copy-start | bytes 1540
  208.1 13.9 %copy-start.4 = (f32[128]{0:T(128)S(1)}, f32[128]{0:T(128)}, u32[]{:S(2)}) copy-start(f32[128]{0:T(128)} %param.10) | copy-start | bytes 1540
  208.1 67.8 %all-gather.4.cloned.1.call-start = ((), (), s32[]{:S(2)}) async-start(), calls=%async_computation.5 | async-start | bytes 5242880 | tf_op jit(solution)/shard_map/all_gather | solution.py:36
  221.9 2.8 copy-start.2
  226.0 254.3 %reduce-scatter.6.cloned.1.call-start = ((), (), s32[]{:S(2)}) async-start(), calls=%async_computation.6 | async-start | bytes 20971520 | tf_op jit(solution)/shard_map/reduce_scatter | solution.py:49
  310.6 218.4 %reduce-scatter.8.cloned.1.call-start = ((), (), s32[]{:S(2)}) async-start(), calls=%async_computation.7 | async-start | bytes 5242880 | tf_op jit(solution)/shard_map/reduce_scatter | solution.py:49
  480.3 76.7 %reduce-scatter.10.cloned.1.call-start = ((), (), s32[]{:S(2)}) async-start(), calls=%async_computation.9 | async-start | bytes 1572864
Sparse Core Ops, SparseCore 0:
  11.1 158.5 all-gather.5
  226.1 49.8 all-gather.3
  310.8 169.4 reduce-scatter.5
  482.6 46.4 reduce-scatter.7
  533.0 23.9 reduce-scatter.9
